TPU v7x, 32 devices: a whole 2x2x4 slice. The times are simulated.
32 devices in a mesh: row: 4 (over y, x), col: 8 (over z, core).
Axes of the slice: x: 2, y: 2, z: 4, core: 2. Of those that a mesh axis runs over, the one named last changes fastest.
Arguments:
- spectra: bfloat16 [16, 2048, 2048], P('row', None, 'col'), may hold values from -6 to 6
- coupling: float32 [16], replicated, may hold values from 0.2 to 1
Outputs:
- returned_spectra: bfloat16 [16, 2048, 2048], P('row', None, 'col')
All inputs are finite; a program needn't handle non-finite values.
Results may differ from a plain program's by a relative error of at most 0.0079.
Values may be sent and summed in bfloat16 or wider, within the bound.
No kernel may reach another device: no remote copies, remote signals or barrier semaphores. Data moves between devices by JAX's collectives and lax.ppermute only.
A program may use at most 128 MiB of HBM per device.

v0:
```python
import math
import jax
import jax.numpy as jnp
from jax import lax
from jax.sharding import PartitionSpec as P

NX = 3072
NY = 3072
M = 1024


def fourier_rows(mode_count, length, factor):
    wavenumber = jnp.arange(1, mode_count + 1, dtype=jnp.int32)
    position = jnp.arange(length, dtype=jnp.int32)
    residue = wavenumber[:, None] * position[None, :] % length
    angles = residue.astype(jnp.float32) * (2.0 * math.pi / length)
    table = jnp.concatenate([jnp.cos(angles), jnp.sin(angles)], 0) * factor
    return table.astype(jnp.bfloat16)


def ellipse(row_index, column_index, mode_count):
    row_waves = row_index % mode_count + 1
    col_waves = column_index % mode_count + 1
    inside = (
        row_waves[:, None] * row_waves[:, None] + col_waves[None, :] * col_waves[None, :]
        <= mode_count * mode_count
    )
    return inside.astype(jnp.float32)


def on_device(spectra, coupling):
    local_count = spectra.shape[0]
    width_here = spectra.shape[2]
    inverse_y = fourier_rows(M, NY, 1.0 / math.sqrt(M)).T
    inverse_x = fourier_rows(M, NX, 1.0 / math.sqrt(M))
    forward_x = fourier_rows(M, NX, 2.0 * math.sqrt(M) / NX).T
    forward_y = fourier_rows(M, NY, 2.0 * math.sqrt(M) / NY)
    half_done = jnp.einsum(
        "yk,fkc->fyc", inverse_y, spectra, preferred_element_type=jnp.float32
    ).astype(jnp.bfloat16)
    gathered = lax.all_to_all(half_done, "col", split_axis=1, concat_axis=2, tiled=True)
    first_field = lax.axis_index("row") * local_count
    strength = lax.dynamic_slice_in_dim(coupling, first_field, gathered.shape[0])
    gridded = jnp.einsum("fyk,kx->fyx", gathered, inverse_x, preferred_element_type=jnp.float32)
    tendency = (gridded + strength[:, None, None] * gridded * gridded).astype(jnp.bfloat16)
    projected = jnp.einsum(
        "fyx,xk->fyk", tendency, forward_x, preferred_element_type=jnp.float32
    ).astype(jnp.bfloat16)
    returned = lax.all_to_all(projected, "col", split_axis=2, concat_axis=1, tiled=True)
    result = jnp.einsum("ky,fyc->fkc", forward_y, returned, preferred_element_type=jnp.float32)
    columns = lax.axis_index("col") * width_here + jnp.arange(width_here, dtype=jnp.int32)
    inside = ellipse(jnp.arange(2 * M, dtype=jnp.int32), columns, M)
    return (result * inside[None, :, :]).astype(jnp.bfloat16)


def solution(mesh):
    placed = (P("row", None, "col"), P())
    return jax.shard_map(
        on_device, mesh=mesh, in_specs=placed, out_specs=P("row", None, "col"), check_vma=False
    )
```

profile of v0, /device:TPU:0, one launch (start us, length us, event | category | flops | bytes accessed | tf_op | source)
XLA Modules:
  0.0 505.0 jit_solution(3590374729908584467)
XLA Ops:
  0.0 52.6 %fusion.8 = (f32[1024,3072]{0,1:T(8,128)}, f32[1024,3072]{0,1:T(8,128)}) fusion(s32[1024]{0:T(1024)S(1)} %iota_add_fusion), kind=kLoop, calls=%fused_computation.14 | loop fusion | flops 28311552 | bytes 25169920 | tf_op jit(solution)/shard_map/cos | solution.py:17
  52.6 20.9 %convert_bitcast_fusion = bf16[4,3072,256]{2,1,0:T(8,128)(2,1)} fusion(bf16[4,2048,256]{2,1,0:T(8,128)(2,1)} %param.2, f32[1024,3072]{0,1:T(8,128)} %get-tuple-element.6, f32[1024,3072]{0,1:T(8,128)} %get-tuple-element.5), kind=kOutput, calls=%fused_computation.23 | convolution fusion | flops 12906921984 | bytes 35651584 | tf_op jit(solution)/shard_map/yk,fkc->fyc/dot_general | solution.py:38
  73.5 0.0 copy-start
  73.5 10.5 %copy.9 = bf16[4,3072,256]{2,0,1:T(4,128)(2,1)} copy(bf16[4,3072,256]{2,1,0:T(8,128)(2,1)} %convert_bitcast_fusion) | data formatting | bytes 12582912 | tf_op jit(solution)/shard_map/convert_element_type | solution.py:40
  84.0 6.4 %all-to-all-start = ((bf16[4,3072,256]{2,0,1:T(4,128)(2,1)}), bf16[4,3072,256]{2,0,1:T(4,128)(2,1)}, u32[]{:S(2)}, u32[]{:S(2)}) async-start(bf16[4,3072,256]{2,0,1:T(4,128)(2,1)} %copy.9), calls=%async_computation | async-start | bytes 12582912 | tf_op jit(solution)/shard_map/all_to_all | solution.py:41
  90.4 0.0 copy-done
  90.4 0.1 dynamic_slice.3
  90.5 138.9 %all-to-all-done = bf16[4,3072,256]{2,0,1:T(4,128)(2,1)} async-done(((bf16[4,3072,256]{2,0,1:T(4,128)(2,1)}), bf16[4,3072,256]{2,0,1:T(4,128)(2,1)}, u32[]{:S(2)}, u32[]{:S(2)}) %all-to-all-start) | async-done | bytes 6291488 | tf_op jit(solution)/shard_map/all_to_all | solution.py:41
  229.4 9.1 %copy.26 = bf16[4,8,384,256]{3,1,2,0:T(8,128)(2,1)} copy(bf16[4,8,384,256]{3,0,2,1:T(4,128)(2,1)} %bitcast.2) | data formatting | bytes 12582912 | tf_op jit(solution)/shard_map/all_to_all | solution.py:41
  238.5 10.4 %all_to_all.29 = bf16[4,384,2048]{2,1,0:T(8,128)(2,1)} reshape(bf16[4,384,8,256]{3,2,1,0:T(8,128)(2,1)} %bitcast.46) | data formatting | bytes 12582912 | tf_op jit(solution)/shard_map/all_to_all | solution.py:41
  248.9 27.8 %fusion.59 = bf16[4,384,3072]{2,1,0:T(8,128)(2,1)} fusion(bf16[4,384,2048]{2,1,0:T(8,128)(2,1)} %all_to_all.29, f32[4]{0:T(128)S(1)} %dynamic_slice.3, f32[1024,3072]{0,1:T(8,128)} %get-tuple-element.6, f32[1024,3072]{0,1:T(8,128)} %get-tuple-element.5), kind=kOutput, calls=%fused_computation.5.clone.clone.clone.clone.2 | convolution fusion | flops 19365101568 | bytes 40894480 | tf_op jit(solution)/shard_map/fyk,kx->fyx/dot_general | solution.py:44
  276.7 27.5 %fusion.16 = bf16[4,384,2048]{2,1,0:T(8,128)(2,1)} fusion(f32[1024,3072]{0,1:T(8,128)} %get-tuple-element.6, f32[1024,3072]{0,1:T(8,128)} %get-tuple-element.5, bf16[4,384,3072]{2,1,0:T(8,128)(2,1)} %fusion.59), kind=kOutput, calls=%fused_computation.24 | convolution fusion | flops 19349372928 | bytes 40894464 | tf_op jit(solution)/shard_map/fyx,xk->fyk/dot_general | solution.py:46
  304.2 10.7 %copy.13 = bf16[4,384,2048]{1,0,2:T(4,128)(2,1)} copy(bf16[4,384,2048]{2,1,0:T(8,128)(2,1)} %fusion.16) | data formatting | bytes 12582912 | tf_op jit(solution)/shard_map/convert_element_type | solution.py:48
  315.0 4.8 all-to-all-start.1
  319.8 0.3 fusion.19
  320.1 138.6 %all-to-all-done.1 = bf16[4,384,2048]{1,0,2:T(4,128)(2,1)} async-done(((bf16[4,384,2048]{1,0,2:T(4,128)(2,1)}), bf16[4,384,2048]{1,0,2:T(4,128)(2,1)}, u32[]{:S(2)}, u32[]{:S(2)}) %all-to-all-start.1) | async-done | bytes 6291488 | tf_op jit(solution)/shard_map/all_to_all | solution.py:49
  458.7 9.2 %copy.25 = bf16[4,384,8,256]{1,2,3,0:T(8,128)(2,1)} copy(bf16[4,384,8,256]{1,0,3,2:T(4,128)(2,1)} %bitcast.6) | data formatting | bytes 12582912 | tf_op jit(solution)/shard_map/all_to_all | solution.py:49
  467.9 10.4 %all_to_all.33 = bf16[4,3072,256]{1,2,0:T(8,128)(2,1)} reshape(bf16[4,8,384,256]{2,1,3,0:T(8,128)(2,1)} %bitcast.47) | data formatting | bytes 12582912 | tf_op jit(solution)/shard_map/all_to_all | solution.py:49
  478.3 20.5 %fusion.15 = bf16[4,2048,256]{1,2,0:T(8,128)(2,1)} fusion(bf16[4,3072,256]{1,2,0:T(8,128)(2,1)} %all_to_all.33, f32[2048,256]{0,1:T(8,128)S(1)} %fusion.19, f32[1024,3072]{0,1:T(8,128)} %get-tuple-element.6, f32[1024,3072]{0,1:T(8,128)} %get-tuple-element.5), kind=kOutput, calls=%fused_computation.20 | convolution fusion | flops 12907970560 | bytes 37748736 | tf_op jit(solution)/shard_map/ky,fyc->fkc/dot_general | solution.py:50
  498.8 6.2 %copy.16 = bf16[4,2048,256]{2,1,0:T(8,128)(2,1)} copy(bf16[4,2048,256]{1,2,0:T(8,128)(2,1)} %fusion.15) | data formatting | bytes 8388608 | tf_op jit(solution)/shard_map/convert_element_type | solution.py:53
  (3 shorter events, 0.0 us)
Async XLA Ops:
  73.5 16.9 %copy-start = (f32[16]{0:T(128)S(1)}, f32[16]{0:T(128)}, u32[]{:S(2)}) copy-start(f32[16]{0:T(128)} %param.3) | copy-start | bytes 196
  84.0 145.4 %all-to-all-start = ((bf16[4,3072,256]{2,0,1:T(4,128)(2,1)}), bf16[4,3072,256]{2,0,1:T(4,128)(2,1)}, u32[]{:S(2)}, u32[]{:S(2)}) async-start(bf16[4,3072,256]{2,0,1:T(4,128)(2,1)} %copy.9), calls=%async_computation | async-start | bytes 12582912 | tf_op jit(solution)/shard_map/all_to_all | solution.py:41
  315.0 143.7 %all-to-all-start.1 = ((bf16[4,384,2048]{1,0,2:T(4,128)(2,1)}), bf16[4,384,2048]{1,0,2:T(4,128)(2,1)}, u32[]{:S(2)}, u32[]{:S(2)}) async-start(bf16[4,384,2048]{1,0,2:T(4,128)(2,1)} %copy.13), calls=%async_computation.1 | async-start | bytes 12582912 | tf_op jit(solution)/shard_map/all_to_all | solution.py:49
where the time goes:
time: 506 us; the launch traced here: 505 us
  waiting for transfers between devices  278 us (55%)
  matrix products  96.8 us (19%)
  local copies, waits for them, and re-layouts  66.6 us (13%)
  other arithmetic  52.9 us (10%)
  starting transfers between devices  11.1 us (2%)
    all_to_all x1, waiting for transfers between devices, on_device(): lax.all_to_all(half_done, 'col', split_axis=1, concat_axis=2, tiled=True)  139 us
    all_to_all x1, waiting for transfers between devices, on_device(): lax.all_to_all(projected, 'col', split_axis=2, concat_axis=1, tiled=True)  139 us
    cos x1, other arithmetic, fourier_rows(): table = jnp.concatenate([jnp.cos(angles), jnp.sin(angles)], 0) * factor  52.6 us
    dot_general x1, matrix products, on_device(): jnp.einsum('fyk,kx->fyx', gathered, inverse_x, preferred_element_type=jnp...  27.8 us
    dot_general x1, matrix products, on_device(): jnp.einsum('fyx,xk->fyk', tendency, forward_x, preferred_element_type=jnp...  27.5 us
    dot_general x1, matrix products, on_device(): jnp.einsum('yk,fkc->fyc', inverse_y, spectra, preferred_element_type=jnp....  20.9 us
    dot_general x1, matrix products, on_device(): jnp.einsum('ky,fyc->fkc', forward_y, returned, preferred_element_type=jnp...  20.5 us
    all_to_all x2, local copies, waits for them, and re-layouts, on_device(): lax.all_to_all(projected, 'col', split_axis=2, concat_axis=1, tiled=True)  19.6 us
  transfers between devices with their start and end apart: 2, of which 2 were waited for; matrix products, arithmetic and copies ran while one was open for 0% of the time, Pallas kernels for 0%

commit v1 on v0

--- a/solution.py
+++ b/solution.py
@@ -46,7 +46,10 @@
     projected = jnp.einsum(
         "fyx,xk->fyk", tendency, forward_x, preferred_element_type=jnp.float32
     ).astype(jnp.bfloat16)
-    returned = lax.all_to_all(projected, "col", split_axis=2, concat_axis=1, tiled=True)
+    returned = jnp.concatenate(
+        lax.all_to_all(jnp.stack(jnp.split(projected, lax.axis_size("col"), axis=2)), "col", 0, 0),
+        axis=1,
+    )
     result = jnp.einsum("ky,fyc->fkc", forward_y, returned, preferred_element_type=jnp.float32)
     columns = lax.axis_index("col") * width_here + jnp.arange(width_here, dtype=jnp.int32)
     inside = ellipse(jnp.arange(2 * M, dtype=jnp.int32), columns, M)

time: 506 us -> 487 us (0.962)
  local copies, waits for them, and re-layouts: 66.6 us -> 50.5 us
    all_to_all x2 -> x0, local copies, waits for them, and re-layouts: 19.6 us -> none  [on_device(): lax.all_to_all(projected, 'col', split_axis=2, concat_axis=1, tiled=True)]
    convert_element_type x1 -> x0, local copies, waits for them, and re-layouts: 10.7 us -> none  [on_device(): projected = jnp.einsum('fyx,xk->fyk', tendency, forward_x, preferred_elem...]
    unnamed x2 -> x9, local copies, waits for them, and re-layouts: 0.01 us -> 7.06 us
    reshape x0 -> x1, local copies, waits for them, and re-layouts: none -> 6.14 us  [on_device(): jnp.concatenate(lax.all_to_all(jnp.stack(jnp.split(projected, lax.axis_si...]
where the time goes in v1:
time: 487 us; the launch traced here: 486 us
  waiting for transfers between devices  277 us (57%)
  matrix products  94.1 us (19%)
  other arithmetic  52.9 us (11%)
  local copies, waits for them, and re-layouts  50.5 us (10%)
  starting transfers between devices  11.5 us (2%)
    all_to_all x1, waiting for transfers between devices, on_device(): lax.all_to_all(half_done, 'col', split_axis=1, concat_axis=2, tiled=True)  139 us
    all_to_all x1, waiting for transfers between devices, on_device(): lax.all_to_all(jnp.stack(jnp.split(projected, lax.axis_size('col'), axis=...  138 us
    cos x1, other arithmetic, fourier_rows(): table = jnp.concatenate([jnp.cos(angles), jnp.sin(angles)], 0) * factor  52.6 us
    dot_general x1, matrix products, on_device(): jnp.einsum('fyk,kx->fyx', gathered, inverse_x, preferred_element_type=jnp...  27.8 us
    dot_general x1, matrix products, on_device(): jnp.einsum('fyx,xk->fyk', tendency, forward_x, preferred_element_type=jnp...  24.9 us
    dot_general x1, matrix products, on_device(): jnp.einsum('yk,fkc->fyc', inverse_y, spectra, preferred_element_type=jnp....  20.9 us
    dot_general x1, matrix products, on_device(): jnp.einsum('ky,fyc->fkc', forward_y, returned, preferred_element_type=jnp...  20.5 us
    all_to_all x2, local copies, waits for them, and re-layouts, on_device(): lax.all_to_all(half_done, 'col', split_axis=1, concat_axis=2, tiled=True)  19.5 us
  transfers between devices with their start and end apart: 2, of which 2 were waited for; matrix products, arithmetic and copies ran while one was open for 0% of the time, Pallas kernels for 0%

profile of v1, /device:TPU:0, one launch (start us, length us, event | category | flops | bytes accessed | tf_op | source)
XLA Modules:
  0.0 486.3 jit_solution(2253539418045676433)
XLA Ops:
  0.0 52.6 %fusion.8 = (f32[1024,3072]{0,1:T(8,128)}, f32[1024,3072]{0,1:T(8,128)}) fusion(s32[1024]{0:T(1024)S(1)} %iota_add_fusion), kind=kLoop, calls=%fused_computation.14 | loop fusion | flops 28311552 | bytes 25169920 | tf_op jit(solution)/shard_map/cos | solution.py:17
  52.6 20.9 %convert_bitcast_fusion = bf16[4,3072,256]{2,1,0:T(8,128)(2,1)} fusion(bf16[4,2048,256]{2,1,0:T(8,128)(2,1)} %param.2, f32[1024,3072]{0,1:T(8,128)} %get-tuple-element.6, f32[1024,3072]{0,1:T(8,128)} %get-tuple-element.5), kind=kOutput, calls=%fused_computation.22 | convolution fusion | flops 12906921984 | bytes 35651584 | tf_op jit(solution)/shard_map/yk,fkc->fyc/dot_general | solution.py:38
  73.5 10.5 %copy.15 = bf16[4,3072,256]{2,0,1:T(4,128)(2,1)} copy(bf16[4,3072,256]{2,1,0:T(8,128)(2,1)} %convert_bitcast_fusion) | data formatting | bytes 12582912 | tf_op jit(solution)/shard_map/convert_element_type | solution.py:40
  84.0 0.0 copy-start
  84.0 6.5 %all-to-all-start = ((bf16[4,3072,256]{2,0,1:T(4,128)(2,1)}), bf16[4,3072,256]{2,0,1:T(4,128)(2,1)}, u32[]{:S(2)}, u32[]{:S(2)}) async-start(bf16[4,3072,256]{2,0,1:T(4,128)(2,1)} %copy.15), calls=%async_computation | async-start | bytes 12582912 | tf_op jit(solution)/shard_map/all_to_all | solution.py:41
  90.5 0.0 copy-done
  90.5 0.1 dynamic_slice.3
  90.6 138.9 %all-to-all-done = bf16[4,3072,256]{2,0,1:T(4,128)(2,1)} async-done(((bf16[4,3072,256]{2,0,1:T(4,128)(2,1)}), bf16[4,3072,256]{2,0,1:T(4,128)(2,1)}, u32[]{:S(2)}, u32[]{:S(2)}) %all-to-all-start) | async-done | bytes 6291488 | tf_op jit(solution)/shard_map/all_to_all | solution.py:41
  229.5 9.1 %copy.31 = bf16[4,8,384,256]{3,1,2,0:T(8,128)(2,1)} copy(bf16[4,8,384,256]{3,0,2,1:T(4,128)(2,1)} %bitcast.2) | data formatting | bytes 12582912 | tf_op jit(solution)/shard_map/all_to_all | solution.py:41
  238.6 10.4 %all_to_all.19 = bf16[4,384,2048]{2,1,0:T(8,128)(2,1)} reshape(bf16[4,384,8,256]{3,2,1,0:T(8,128)(2,1)} %bitcast.72) | data formatting | bytes 12582912 | tf_op jit(solution)/shard_map/all_to_all | solution.py:41
  249.0 27.8 %fusion.67 = bf16[4,384,3072]{2,1,0:T(8,128)(2,1)} fusion(bf16[4,384,2048]{2,1,0:T(8,128)(2,1)} %all_to_all.19, f32[4]{0:T(128)S(1)} %dynamic_slice.3, f32[1024,3072]{0,1:T(8,128)} %get-tuple-element.6, f32[1024,3072]{0,1:T(8,128)} %get-tuple-element.5), kind=kOutput, calls=%fused_computation.5.clone.clone.clone.clone.2 | convolution fusion | flops 19365101568 | bytes 40894480 | tf_op jit(solution)/shard_map/fyk,kx->fyx/dot_general | solution.py:44
  276.8 24.9 %fusion.16 = bf16[4,384,2048]{2,1,0:T(8,128)(2,1)S(1)} fusion(f32[1024,3072]{0,1:T(8,128)} %get-tuple-element.6, f32[1024,3072]{0,1:T(8,128)} %get-tuple-element.5, bf16[4,384,3072]{2,1,0:T(8,128)(2,1)} %fusion.67), kind=kOutput, calls=%fused_computation.23 | convolution fusion | flops 19349372928 | bytes 40894464 | tf_op jit(solution)/shard_map/fyx,xk->fyk/dot_general | solution.py:46
  301.7 1.0 fusion.32
  302.7 1.0 fusion.31
  303.7 1.0 fusion.30
  304.7 1.0 fusion.29
  305.7 1.0 fusion.28
  306.7 1.0 fusion.27
  307.7 1.0 fusion.26
  308.8 1.0 fusion.25
  309.8 5.0 %all-to-all-start.1 = ((bf16[8,4,384,256]{3,2,1,0:T(8,128)(2,1)}), bf16[8,4,384,256]{3,2,1,0:T(8,128)(2,1)}, u32[]{:S(2)}, u32[]{:S(2)}) async-start(bf16[8,4,384,256]{3,2,1,0:T(8,128)(2,1)} %fusion.25), calls=%async_computation.1 | async-start | bytes 12582912 | tf_op jit(solution)/shard_map/all_to_all | solution.py:50
  314.8 0.3 fusion.19
  315.1 138.3 %all-to-all-done.1 = bf16[8,4,384,256]{3,2,1,0:T(8,128)(2,1)} async-done(((bf16[8,4,384,256]{3,2,1,0:T(8,128)(2,1)}), bf16[8,4,384,256]{3,2,1,0:T(8,128)(2,1)}, u32[]{:S(2)}, u32[]{:S(2)}) %all-to-all-start.1) | async-done | bytes 6291488 | tf_op jit(solution)/shard_map/all_to_all | solution.py:50
  453.4 6.1 %copy.19 = bf16[4,8,384,256]{3,2,1,0:T(8,128)(2,1)} copy(bf16[4,8,384,256]{3,2,0,1:T(8,128)(2,1)} %bitcast.14) | data formatting | bytes 12582912 | tf_op jit(solution)/shard_map/reshape | solution.py:49
  459.6 20.5 %fusion.15 = bf16[4,2048,256]{1,2,0:T(8,128)(2,1)} fusion(bf16[4,3072,256]{2,1,0:T(8,128)(2,1)} %bitcast.73, f32[2048,256]{0,1:T(8,128)S(1)} %fusion.19, f32[1024,3072]{0,1:T(8,128)} %get-tuple-element.6, f32[1024,3072]{0,1:T(8,128)} %get-tuple-element.5), kind=kOutput, calls=%fused_computation.20 | convolution fusion | flops 12907970560 | bytes 37748736 | tf_op jit(solution)/shard_map/ky,fyc->fkc/dot_general | solution.py:53
  480.1 6.2 %copy.22 = bf16[4,2048,256]{2,1,0:T(8,128)(2,1)} copy(bf16[4,2048,256]{1,2,0:T(8,128)(2,1)} %fusion.15) | data formatting | bytes 8388608 | tf_op jit(solution)/shard_map/convert_element_type | solution.py:56
  (3 shorter events, 0.0 us)
Async XLA Ops:
  84.0 6.5 %copy-start = (f32[16]{0:T(128)S(1)}, f32[16]{0:T(128)}, u32[]{:S(2)}) copy-start(f32[16]{0:T(128)} %param.3) | copy-start | bytes 196
  84.0 145.5 %all-to-all-start = ((bf16[4,3072,256]{2,0,1:T(4,128)(2,1)}), bf16[4,3072,256]{2,0,1:T(4,128)(2,1)}, u32[]{:S(2)}, u32[]{:S(2)}) async-start(bf16[4,3072,256]{2,0,1:T(4,128)(2,1)} %copy.15), calls=%async_computation | async-start | bytes 12582912 | tf_op jit(solution)/shard_map/all_to_all | solution.py:41
  309.8 143.7 %all-to-all-start.1 = ((bf16[8,4,384,256]{3,2,1,0:T(8,128)(2,1)}), bf16[8,4,384,256]{3,2,1,0:T(8,128)(2,1)}, u32[]{:S(2)}, u32[]{:S(2)}) async-start(bf16[8,4,384,256]{3,2,1,0:T(8,128)(2,1)} %fusion.25), calls=%async_computation.1 | async-start | bytes 12582912 | tf_op jit(solution)/shard_map/all_to_all | solution.py:50
